TPU v7x, 256 devices: a whole 4x4x8 slice. The times are simulated.
256 devices in a mesh: dp: 32 (over y, x, core), seq: 8 (over z).
Axes of the slice: x: 4, y: 4, z: 8, core: 2. Of those that a mesh axis runs over, the one named last changes fastest.
Arguments:
- query_rows: bfloat16 [32, 1024, 3072], P('dp', 'seq'), may hold values from -6 to 6
- key_rows: bfloat16 [32, 1024, 3072], P('dp', 'seq'), may hold values from -6 to 6
- value_rows: bfloat16 [32, 1024, 3072], P('dp', 'seq'), may hold values from -6 to 6
- out_grad: bfloat16 [32, 1024, 6144], P('dp', 'seq'), may hold values from -54 to 54
- clip_lengths: int32 [32, 4], P('dp'), may hold values from 1 to 512, 1024 in all within a row
- out_weight: bfloat16 [3072, 6144], P('seq'), may hold values from -0.109375 to 0.109375
- query_gain: float32 [128], replicated, may hold values from 0.1 to 1.9
- key_gain: float32 [128], replicated, may hold values from 0.1 to 1.9
Outputs:
- query_grad: bfloat16 [32, 1024, 3072], P('dp', 'seq')
- key_grad: bfloat16 [32, 1024, 3072], P('dp', 'seq')
- value_grad: bfloat16 [32, 1024, 3072], P('dp', 'seq')
- weight_grad: float32 [3072, 6144], P('seq', 'dp')
- querygain_grad: float32 [128], replicated
- keygain_grad: float32 [128], replicated
- grad_norm: float32 [], replicated
Inputs may be any that keep to these rules, and one draw needn't show every extreme that they name: `clip_lengths`: the token counts of each group's clips sum to 1024.
All inputs are finite; a program needn't handle non-finite values.
Results may differ from a plain program's by a relative error of at most 0.015.
Values may be sent and summed in bfloat16 or wider, within the bound.
A program may use at most 128 MiB of HBM per device.

v0:
```python
import jax
import jax.numpy as jnp
from jax import lax
from jax.sharding import Mesh
from jax.sharding import PartitionSpec as P

HEAD_DIM = 128
MAX_NORM = 768
DP = ("dp_0", "dp_1", "dp_2")
DP_SEQ = ("dp_0", "dp_1", "dp_2", "seq")
EPS = 1e-06


def one_axis_at_a_time(array, axes):
    for axis in axes:
        array = lax.psum(array, axis)
    return array


def segment_ids(lengths, total):
    ends = jnp.cumsum(lengths)
    places = jnp.arange(total, dtype=jnp.int32)
    return jnp.sum((places[:, None] >= ends[None, :]).astype(jnp.int32), axis=1)


def norm_rows(rows, gain):
    wide = rows.astype(jnp.float32)
    inverse = lax.rsqrt(jnp.mean(wide * wide, axis=-1, keepdims=True) + EPS)
    unit = wide * inverse
    return (unit, inverse, (unit * gain).astype(jnp.bfloat16))


def norm_back(unit, inverse, gain, d_norm):
    gain_part = jnp.sum(unit * d_norm, axis=(0, 1))
    d_unit = d_norm * gain
    d_rows = inverse * (d_unit - unit * jnp.mean(unit * d_unit, axis=-1, keepdims=True))
    return (d_rows.astype(jnp.bfloat16), gain_part)


def local(
    query_rows, key_rows, value_rows, out_grad, clip_lengths, out_weight, query_gain, key_gain
):
    query, keys, values = (
        lax.all_to_all(query_rows[0], "seq", split_axis=1, concat_axis=0, tiled=True),
        lax.all_to_all(key_rows[0], "seq", split_axis=1, concat_axis=0, tiled=True),
        lax.all_to_all(value_rows[0], "seq", split_axis=1, concat_axis=0, tiled=True),
    )
    total = query.shape[0]
    heads = query.shape[1] // HEAD_DIM
    width = heads * HEAD_DIM
    scale = HEAD_DIM ** (-0.5)
    block = min(512, total)
    blocks = total // block
    seg = segment_ids(clip_lengths[0], total)
    q_unit, q_inv, q_norm = norm_rows(query.reshape(total, heads, HEAD_DIM), query_gain)
    k_unit, k_inv, k_norm = norm_rows(keys.reshape(total, heads, HEAD_DIM), key_gain)
    values3 = values.reshape(total, heads, HEAD_DIM)

    def forward_block(index):
        start = index * block
        query_block = lax.dynamic_slice_in_dim(q_norm, start, block, 0)
        seg_block = lax.dynamic_slice_in_dim(seg, start, block, 0)
        scores = (
            jnp.einsum("qhd,khd->hqk", query_block, k_norm, preferred_element_type=jnp.float32)
            * scale
        )
        same = seg_block[:, None] == seg[None, :]
        expo = jnp.where(same[None], jnp.exp(scores), 0.0)
        probs = (expo / jnp.sum(expo, axis=-1, keepdims=True)).astype(jnp.bfloat16)
        attn_out = jnp.einsum("hqk,khd->qhd", probs, values3, preferred_element_type=jnp.float32)
        return (probs, attn_out.astype(jnp.bfloat16))

    probs_all, attn_blocks = lax.map(forward_block, jnp.arange(blocks, dtype=jnp.int32))
    attn_flat = attn_blocks.reshape(total, width)
    out_full = lax.all_gather(out_grad[0], "seq", axis=0, tiled=True)
    weight_part = jnp.dot(attn_flat.T, out_full, preferred_element_type=jnp.float32)
    d_attn = jnp.dot(out_full, out_weight.T, preferred_element_type=jnp.float32).astype(
        jnp.bfloat16
    )
    d_attn3 = d_attn.reshape(total, heads, HEAD_DIM)

    def backward_block(carry, items):
        d_key, d_value = carry
        probs, index = items
        start = index * block
        attn_grad = lax.dynamic_slice_in_dim(d_attn3, start, block, 0)
        query_block = lax.dynamic_slice_in_dim(q_norm, start, block, 0)
        d_probs = jnp.einsum("qhd,khd->hqk", attn_grad, values3, preferred_element_type=jnp.float32)
        probs32 = probs.astype(jnp.float32)
        row_sum = jnp.sum(probs32 * d_probs, axis=-1, keepdims=True)
        d_scores = (probs32 * (d_probs - row_sum) * scale).astype(jnp.bfloat16)
        d_value = d_value + jnp.einsum(
            "hqk,qhd->khd", probs, attn_grad, preferred_element_type=jnp.float32
        )
        d_key = d_key + jnp.einsum(
            "hqk,qhd->khd", d_scores, query_block, preferred_element_type=jnp.float32
        )
        d_query = jnp.einsum("hqk,khd->qhd", d_scores, k_norm, preferred_element_type=jnp.float32)
        return ((d_key, d_value), d_query)

    empty = jnp.zeros((total, heads, HEAD_DIM), jnp.float32)
    (d_knorm, d_value32), d_query_blocks = lax.scan(
        backward_block, (empty, empty), (probs_all, jnp.arange(blocks, dtype=jnp.int32))
    )
    d_qnorm = d_query_blocks.reshape(total, heads, HEAD_DIM)
    query_grad, q_gain_part = norm_back(q_unit, q_inv, query_gain, d_qnorm)
    key_grad, k_gain_part = norm_back(k_unit, k_inv, key_gain, d_knorm)
    value_grad = d_value32.astype(jnp.bfloat16)
    query_back, key_back, value_back = (
        lax.all_to_all(
            query_grad.reshape(total, width), "seq", split_axis=0, concat_axis=1, tiled=True
        ),
        lax.all_to_all(
            key_grad.reshape(total, width), "seq", split_axis=0, concat_axis=1, tiled=True
        ),
        lax.all_to_all(
            value_grad.reshape(total, width), "seq", split_axis=0, concat_axis=1, tiled=True
        ),
    )
    weight_shard = lax.psum_scatter(
        weight_part.astype(jnp.bfloat16), DP, scatter_dimension=1, tiled=True
    ).astype(jnp.float32)
    local_squares = jnp.sum(weight_shard * weight_shard)
    qgain_raw, kgain_raw = (
        one_axis_at_a_time(q_gain_part, DP_SEQ),
        one_axis_at_a_time(k_gain_part, DP_SEQ),
    )
    weight_squares = one_axis_at_a_time(local_squares, DP_SEQ)
    squares = weight_squares + jnp.sum(qgain_raw * qgain_raw) + jnp.sum(kgain_raw * kgain_raw)
    grad_norm = jnp.sqrt(squares)
    factor = jnp.minimum(jnp.float32(1.0), MAX_NORM / (grad_norm + EPS))
    return (
        query_back[None],
        key_back[None],
        value_back[None],
        weight_shard * factor,
        qgain_raw * factor,
        kgain_raw * factor,
        grad_norm,
    )


def solution(mesh):
    torus = Mesh(mesh.devices.reshape(4, 4, 2, mesh.shape["seq"]), ("dp_0", "dp_1", "dp_2", "seq"))
    return jax.shard_map(
        local,
        mesh=torus,
        in_specs=(
            P(DP, "seq", None),
            P(DP, "seq", None),
            P(DP, "seq", None),
            P(DP, "seq", None),
            P(DP, None),
            P("seq", None),
            P(),
            P(),
        ),
        out_specs=(
            P(DP, "seq", None),
            P(DP, "seq", None),
            P(DP, "seq", None),
            P("seq", DP),
            P(),
            P(),
            P(),
        ),
        check_vma=False,
    )
```

profile of v0, /device:TPU:32, one launch (start us, length us, event | category | flops | bytes accessed | tf_op | source)
XLA Modules:
  0.0 430.5 jit_solution(6281215837916845542)
XLA Ops:
  9.5 8.6 %all-to-all-start = ((bf16[128,8,384]{0,2,1:T(8,128)(2,1)}), bf16[128,8,384]{0,2,1:T(8,128)(2,1)S(1)}, u32[]{:S(2)}, u32[]{:S(2)}) async-start(bf16[128,8,384]{0,2,1:T(8,128)(2,1)} %bitcast.4), calls=%async_computation | async-start | bytes 1572864 | tf_op jit(solution)/shard_map/all_to_all | solution.py:44
  19.2 26.2 %all-to-all-done = bf16[128,8,384]{0,2,1:T(8,128)(2,1)S(1)} async-done(((bf16[128,8,384]{0,2,1:T(8,128)(2,1)}), bf16[128,8,384]{0,2,1:T(8,128)(2,1)S(1)}, u32[]{:S(2)}, u32[]{:S(2)}) %all-to-all-start) | async-done | bytes 786464 | tf_op jit(solution)/shard_map/all_to_all | solution.py:44
  45.4 5.8 %all-to-all-start.1 = ((bf16[128,8,384]{0,2,1:T(8,128)(2,1)}), bf16[128,8,384]{0,2,1:T(8,128)(2,1)S(1)}, u32[]{:S(2)}, u32[]{:S(2)}) async-start(bf16[128,8,384]{0,2,1:T(8,128)(2,1)} %bitcast.8), calls=%async_computation.1 | async-start | bytes 1572864 | tf_op jit(solution)/shard_map/all_to_all | solution.py:45
  52.3 30.0 %all-to-all-done.1 = bf16[128,8,384]{0,2,1:T(8,128)(2,1)S(1)} async-done(((bf16[128,8,384]{0,2,1:T(8,128)(2,1)}), bf16[128,8,384]{0,2,1:T(8,128)(2,1)S(1)}, u32[]{:S(2)}, u32[]{:S(2)}) %all-to-all-start.1) | async-done | bytes 786464 | tf_op jit(solution)/shard_map/all_to_all | solution.py:45
  82.4 5.3 %all-to-all-start.2 = ((bf16[128,8,384]{0,2,1:T(8,128)(2,1)}), bf16[128,8,384]{0,2,1:T(8,128)(2,1)}, u32[]{:S(2)}, u32[]{:S(2)}) async-start(bf16[128,8,384]{0,2,1:T(8,128)(2,1)} %bitcast.10), calls=%async_computation.2 | async-start | bytes 1572864 | tf_op jit(solution)/shard_map/all_to_all | solution.py:46
  89.1 1.6 reshape.182
  90.7 1.2 convert_bitcast_fusion
  92.0 2.1 copy.147
  94.1 1.5 reshape.183
  97.4 2.3 copy.151
  99.7 19.1 %all-to-all-done.2 = bf16[128,8,384]{0,2,1:T(8,128)(2,1)} async-done(((bf16[128,8,384]{0,2,1:T(8,128)(2,1)}), bf16[128,8,384]{0,2,1:T(8,128)(2,1)}, u32[]{:S(2)}, u32[]{:S(2)}) %all-to-all-start.2) | async-done | bytes 786464 | tf_op jit(solution)/shard_map/all_to_all | solution.py:46
  118.7 2.5 copy.149
  121.2 2.2 reshape.177
  123.4 2.3 copy.152
  125.7 1.7 multiply_reduce_fusion.5
  128.8 21.1 %while.27 = (s32[]{:T(128)}, bf16[2,3,512,1024]{3,2,1,0:T(8,128)(2,1)}, bf16[2,512,3,128]{3,1,2,0:T(8,128)(2,1)}, s32[2]{0:T(128)S(1)}, s32[1024]{0:T(1024)S(1)}...) while((s32[]{:T(128)}, ...), condition=%wide.region_6.7_spmd, body=%wide.region_4.6_spmd.sunk | while | flops 817035776 | bytes 85746000 | solution.py:73
  130.5 3.4 fusion.75
  134.0 1.9 bitcast_dynamic-update-slice_fusion.2
  137.0 1.5 copy-done.1
  141.1 3.4 fusion.75
  144.5 1.9 bitcast_dynamic-update-slice_fusion.2
  147.6 1.5 copy-done.1
  149.9 3.1 copy.167
  153.0 2.1 copy.180
  155.3 1.5 copy.176
  156.8 32.1 %all-gather.3.cloned.1.call-done = bf16[1,1024,6144]{2,1,0:T(8,128)(2,1)} async-done(((bf16[1,128,6144]{2,1,0:T(8,128)(2,1)}), bf16[1,1024,6144]{2,1,0:T(8,128)(2,1)}) %all-gather.3.cloned.1.call-update) | async-done | bytes 12582928 | tf_op jit(solution)/shard_map/all_gather | solution.py:75
  188.9 11.4 %fusion.42 = bf16[384,6144]{0,1:T(8,128)(2,1)} fusion(bf16[1024,384]{0,1:T(8,128)(2,1)} %bitcast.161, bf16[1,1024,6144]{2,1,0:T(8,128)(2,1)} %all-gather.3.cloned.1.call-done), kind=kOutput, calls=%fused_computation.45 | convolution fusion | flops 4834197504 | bytes 18087936 | tf_op jit(solution)/shard_map/dot_general | solution.py:76
  200.3 10.4 %fusion.48 = bf16[1024,384]{0,1:T(8,128)(2,1)} fusion(bf16[384,6144]{1,0:T(8,128)(2,1)} %param.17, bf16[1,1024,6144]{2,1,0:T(8,128)(2,1)} %all-gather.3.cloned.1.call-done), kind=kOutput, calls=%fused_computation.62 | convolution fusion | flops 4832231424 | bytes 18087936 | tf_op jit(solution)/shard_map/dot_general | solution.py:77
  210.8 57.7 %while.28 = (s32[]{:T(128)}, f32[1024,3,128]{0,2,1:T(8,128)}, f32[1024,3,128]{0,2,1:T(8,128)S(1)}, f32[2,512,3,128]{3,1,2,0:T(8,128)}, s32[2]{0:T(128)S(1)}, /*i...) while((s32[]{:T(128)}, f32[1024,3,128]{0,2,1:T(8,128)}, ...), condition=%wide.region_9.10_spmd.clone, body=%wide.region_7.9_spmd.clone.sunk | while | flops 1634210816 | bytes 57019604 | solution.py:102
  212.0 5.0 %fusion.83 = f32[3,512,1024]{2,1,0:T(8,128)} fusion(bf16[1024,3,128]{2,0,1:T(8,128)(2,1)} %get-tuple-element.549, bf16[1024,3,128]{0,2,1:T(8,128)(2,1)} %get-tuple-element.548, s32[]{:T(128)S(6)} %select_n.24), kind=kOutput, calls=%fused_computation.30.clone.1 | convolution fusion | flops 402653184 | bytes 7471108 | tf_op jit(solution)/shard_map/while/body/eval_jaxpr/qhd,khd->hqk/dot_general | solution.py:88
  217.0 10.2 %bitcast_add_fusion.4 = f32[1024,3,128]{0,2,1:T(8,128)} fusion(f32[1024,3,128]{0,2,1:T(8,128)} %get-tuple-element.528, f32[3,512,1024]{2,1,0:T(8,128)} %fusion.83, bf16[2,3,512,1024]{3,2,1,0:T(8,128)(2,1)} %get-tuple-element.547, s32[]{:T(128)} %get-tuple-element.527, pred[]{:T(512)S(6)} %compare.3, bf16[1024,3,128]{0,2,1:T(8,128)(2,1)} %get-tuple-element.546, ...), kind=kOutput, calls=%fused_computation.26.clone.1 | convolution fusion | flops 414452224 | bytes 22414340 | tf_op jit(solution)/shard_map/while/body/eval_jaxpr/hqk,qhd->khd/dot_general | solution.py:95
  227.2 9.7 %fusion.84 = f32[2,512,3,128]{3,1,2,0:T(8,128)} fusion(f32[2,512,3,128]{3,1,2,0:T(8,128)} %get-tuple-element.530, s32[]{:T(128)} %get-tuple-element.527, bf16[1024,3,128]{2,0,1:T(8,128)(2,1)} %get-tuple-element.550, f32[3,512,1024]{2,1,0:T(8,128)} %fusion.83, bf16[2,3,512,1024]{3,2,1,0:T(8,128)(2,1)} %get-tuple-element.547), kind=kOutput, calls=%fused_computation.28.clone.1 | convolution fusion | flops 413665792 | bytes 20448768 | tf_op jit(solution)/shard_map/while/body/eval_jaxpr/hqk,khd->qhd/dot_general | solution.py:98
  236.9 3.0 bitcast_add_fusion.5
  241.2 4.9 %fusion.83 = f32[3,512,1024]{2,1,0:T(8,128)} fusion(bf16[1024,3,128]{2,0,1:T(8,128)(2,1)} %get-tuple-element.549, bf16[1024,3,128]{0,2,1:T(8,128)(2,1)} %get-tuple-element.548, s32[]{:T(128)S(6)} %select_n.24), kind=kOutput, calls=%fused_computation.30.clone.1 | convolution fusion | flops 402653184 | bytes 7471108 | tf_op jit(solution)/shard_map/while/body/eval_jaxpr/qhd,khd->hqk/dot_general | solution.py:88
  246.1 10.1 %bitcast_add_fusion.4 = f32[1024,3,128]{0,2,1:T(8,128)} fusion(f32[1024,3,128]{0,2,1:T(8,128)} %get-tuple-element.528, f32[3,512,1024]{2,1,0:T(8,128)} %fusion.83, bf16[2,3,512,1024]{3,2,1,0:T(8,128)(2,1)} %get-tuple-element.547, s32[]{:T(128)} %get-tuple-element.527, pred[]{:T(512)S(6)} %compare.3, bf16[1024,3,128]{0,2,1:T(8,128)(2,1)} %get-tuple-element.546, ...), kind=kOutput, calls=%fused_computation.26.clone.1 | convolution fusion | flops 414452224 | bytes 22414340 | tf_op jit(solution)/shard_map/while/body/eval_jaxpr/hqk,qhd->khd/dot_general | solution.py:95
  256.2 9.3 %fusion.84 = f32[2,512,3,128]{3,1,2,0:T(8,128)} fusion(f32[2,512,3,128]{3,1,2,0:T(8,128)} %get-tuple-element.530, s32[]{:T(128)} %get-tuple-element.527, bf16[1024,3,128]{2,0,1:T(8,128)(2,1)} %get-tuple-element.550, f32[3,512,1024]{2,1,0:T(8,128)} %fusion.83, bf16[2,3,512,1024]{3,2,1,0:T(8,128)(2,1)} %get-tuple-element.547), kind=kOutput, calls=%fused_computation.28.clone.1 | convolution fusion | flops 413665792 | bytes 20448768 | tf_op jit(solution)/shard_map/while/body/eval_jaxpr/hqk,khd->qhd/dot_general | solution.py:98
  265.5 2.9 bitcast_add_fusion.5
  268.5 3.7 copy.156
  272.2 2.7 copy.159
  274.9 3.0 copy.160
  277.9 2.3 multiply_reduce_fusion.3
  280.4 1.6 copy.177
  281.9 3.3 reshape.179
  285.3 4.3 fusion.47
  289.5 6.7 %all-to-all-start.3 = ((bf16[8,128,384]{1,2,0:T(8,128)(2,1)}), bf16[8,128,384]{1,2,0:T(8,128)(2,1)}, u32[]{:S(2)}, u32[]{:S(2)}) async-start(bf16[8,128,384]{1,2,0:T(8,128)(2,1)} %fusion.47), calls=%async_computation.3 | async-start | bytes 1572864 | tf_op jit(solution)/shard_map/all_to_all | solution.py:110
  296.2 2.0 multiply_reduce_fusion
  298.9 1.4 copy.163
  300.3 17.9 %all-to-all-done.3 = bf16[8,128,384]{1,2,0:T(8,128)(2,1)} async-done(((bf16[8,128,384]{1,2,0:T(8,128)(2,1)}), bf16[8,128,384]{1,2,0:T(8,128)(2,1)}, u32[]{:S(2)}, u32[]{:S(2)}) %all-to-all-start.3) | async-done | bytes 786464 | tf_op jit(solution)/shard_map/all_to_all | solution.py:110
  318.2 4.9 %all-to-all-start.4 = ((bf16[8,128,384]{2,1,0:T(8,128)(2,1)}), bf16[8,128,384]{2,1,0:T(8,128)(2,1)S(1)}, u32[]{:S(2)}, u32[]{:S(2)}) async-start(bf16[8,128,384]{2,1,0:T(8,128)(2,1)} %copy.163), calls=%async_computation.4 | async-start | bytes 1572864 | tf_op jit(solution)/shard_map/all_to_all | solution.py:113
  323.4 1.4 copy.165
  324.8 18.6 %all-to-all-done.4 = bf16[8,128,384]{2,1,0:T(8,128)(2,1)S(1)} async-done(((bf16[8,128,384]{2,1,0:T(8,128)(2,1)}), bf16[8,128,384]{2,1,0:T(8,128)(2,1)S(1)}, u32[]{:S(2)}, u32[]{:S(2)}) %all-to-all-start.4) | async-done | bytes 786464 | tf_op jit(solution)/shard_map/all_to_all | solution.py:113
  343.4 5.5 %all-to-all-start.5 = ((bf16[8,128,384]{2,1,0:T(8,128)(2,1)}), bf16[8,128,384]{2,1,0:T(8,128)(2,1)}, u32[]{:S(2)}, u32[]{:S(2)}) async-start(bf16[8,128,384]{2,1,0:T(8,128)(2,1)} %copy.165), calls=%async_computation.5 | async-start | bytes 1572864 | tf_op jit(solution)/shard_map/all_to_all | solution.py:116
  349.0 1.9 reshape.184
  350.9 2.6 multiply_reduce_fusion.1
  353.6 2.4 copy.170
  356.3 1.2 copy.171
  357.5 11.9 %all-to-all-done.5 = bf16[8,128,384]{2,1,0:T(8,128)(2,1)} async-done(((bf16[8,128,384]{2,1,0:T(8,128)(2,1)}), bf16[8,128,384]{2,1,0:T(8,128)(2,1)}, u32[]{:S(2)}, u32[]{:S(2)}) %all-to-all-start.5) | async-done | bytes 786464 | tf_op jit(solution)/shard_map/all_to_all | solution.py:116
  369.4 1.5 copy.166
  372.1 1.6 fusion.51
  373.6 13.2 %all-reduce.2 = (f32[]{:T(128)}, f32[128]{0:T(128)S(1)}, f32[128]{0:T(128)S(1)}) all-reduce(f32[]{:T(128)} %fusion.51, f32[128]{0:T(128)S(1)} %multiply_reduce_fusion.1, f32[128]{0:T(128)S(1)} %get-tuple-element.303), channel_id=1, replica_groups=mesh['dp_0'=4,'dp_1'=4,'dp_2'=2,'seq'=8] {'dp_0'}, use_global_device_ids=true, to_apply=%region_14.15 | all-reduce | flops 257 | bytes 2056 | tf_op jit(solution)/shard_map/psum | solution.py:16
  386.9 11.0 %all-reduce.1 = (f32[]{:T(128)}, f32[128]{0:T(128)S(1)}, f32[128]{0:T(128)S(1)}) all-reduce(f32[]{:T(128)} %get-tuple-element.347, f32[128]{0:T(128)S(1)} %get-tuple-element.348, f32[128]{0:T(128)S(1)} %get-tuple-element.349), channel_id=1, replica_groups=mesh['dp_0'=4,'dp_1'=4,'dp_2'=2,'seq'=8] {'dp_1'}, use_global_device_ids=true, to_apply=%region_15.16 | all-reduce | flops 257 | bytes 2056 | tf_op jit(solution)/shard_map/psum | solution.py:16
  397.9 3.1 all-reduce.3
  401.0 16.2 %all-reduce = (f32[]{:T(128)}, f32[128]{0:T(128)S(1)}, f32[128]{0:T(128)S(1)}) all-reduce(f32[]{:T(128)} %get-tuple-element.350, f32[128]{0:T(128)S(1)} %get-tuple-element.351, f32[128]{0:T(128)S(1)} %get-tuple-element.352), channel_id=1, replica_groups=mesh['dp_0'=4,'dp_1'=4,'dp_2'=2,'seq'=8] {'seq'}, use_global_device_ids=true, to_apply=%region_17.18 | all-reduce | flops 257 | bytes 2056 | tf_op jit(solution)/shard_map/psum | solution.py:16
  420.8 1.6 convert_multiply_fusion.15
  (97 shorter events, 20.7 us)
Async XLA Ops:
  7.2 1.1 copy-start.12
  7.2 181.7 %all-gather.3.cloned.1.call-start = ((), (), s32[]{:S(2)}) async-start(), calls=%async_computation.8 | async-start | bytes 14155776 | tf_op jit(solution)/shard_map/all_gather | solution.py:75
  8.3 9.7 %copy-start.13 = (bf16[1,128,3072]{2,1,0:T(8,128)(2,1)S(1)}, bf16[1,128,3072]{2,1,0:T(8,128)(2,1)}, u32[]{:S(2)}) copy-start(bf16[1,128,3072]{2,1,0:T(8,128)(2,1)} %param.13) | copy-start | bytes 2359300
  9.5 35.9 %all-to-all-start = ((bf16[128,8,384]{0,2,1:T(8,128)(2,1)}), bf16[128,8,384]{0,2,1:T(8,128)(2,1)S(1)}, u32[]{:S(2)}, u32[]{:S(2)}) async-start(bf16[128,8,384]{0,2,1:T(8,128)(2,1)} %bitcast.4), calls=%async_computation | async-start | bytes 1572864 | tf_op jit(solution)/shard_map/all_to_all | solution.py:44
  18.0 33.2 %copy-start.14 = (bf16[1,128,3072]{2,1,0:T(8,128)(2,1)S(1)}, bf16[1,128,3072]{2,1,0:T(8,128)(2,1)}, u32[]{:S(2)}) copy-start(bf16[1,128,3072]{2,1,0:T(8,128)(2,1)} %param.14) | copy-start | bytes 2359300
  45.4 42.6 %copy-start.7 = (bf16[128,8,384]{0,2,1:T(8,128)(2,1)}, bf16[128,8,384]{0,2,1:T(8,128)(2,1)S(1)}, u32[]{:S(2)}) copy-start(bf16[128,8,384]{0,2,1:T(8,128)(2,1)S(1)} %all-to-all-done) | copy-start | bytes 2359300
  45.4 37.0 %all-to-all-start.1 = ((bf16[128,8,384]{0,2,1:T(8,128)(2,1)}), bf16[128,8,384]{0,2,1:T(8,128)(2,1)S(1)}, u32[]{:S(2)}, u32[]{:S(2)}) async-start(bf16[128,8,384]{0,2,1:T(8,128)(2,1)} %bitcast.8), calls=%async_computation.1 | async-start | bytes 1572864 | tf_op jit(solution)/shard_map/all_to_all | solution.py:45
  51.2 36.5 %copy-start.18 = (f32[128]{0:T(128)S(1)}, f32[128]{0:T(128)}, u32[]{:S(2)}) copy-start(f32[128]{0:T(128)} %param.18) | copy-start | bytes 1540
  51.2 36.5 %copy-start.19 = (s32[1,4]{1,0:T(1,128)S(1)}, s32[1,4]{1,0:T(1,128)}, u32[]{:S(2)}) copy-start(s32[1,4]{1,0:T(1,128)} %param.16) | copy-start | bytes 52
  82.4 5.6 %copy-start.11 = (bf16[128,8,384]{0,2,1:T(8,128)(2,1)}, bf16[128,8,384]{0,2,1:T(8,128)(2,1)S(1)}, u32[]{:S(2)}) copy-start(bf16[128,8,384]{0,2,1:T(8,128)(2,1)S(1)} %all-to-all-done.1) | copy-start | bytes 2359300
  82.4 36.3 %all-to-all-start.2 = ((bf16[128,8,384]{0,2,1:T(8,128)(2,1)}), bf16[128,8,384]{0,2,1:T(8,128)(2,1)}, u32[]{:S(2)}, u32[]{:S(2)}) async-start(bf16[128,8,384]{0,2,1:T(8,128)(2,1)} %bitcast.10), calls=%async_computation.2 | async-start | bytes 1572864 | tf_op jit(solution)/shard_map/all_to_all | solution.py:46
  87.7 284.4 %reduce-scatter.2.cloned.1.call-start = ((), (), s32[]{:S(2)}) async-start(), calls=%async_computation.7 | async-start | bytes 4866048 | tf_op jit(solution)/shard_map/reduce_scatter | solution.py:120
  89.0 1.7 copy-start.4
  95.6 0.7 copy-start.17
  125.7 1.9 copy-start.3
  130.5 3.5 copy-start
  134.0 1.9 copy-start.2
  134.0 1.9 copy-start.15
  135.9 2.6 copy-start.1
  138.5 0.9 copy-start.16
  141.1 3.5 copy-start
  144.5 1.9 copy-start.2
  144.5 1.9 copy-start.15
  146.5 2.6 copy-start.1
  149.1 0.9 copy-start.16
  289.5 28.7 %all-to-all-start.3 = ((bf16[8,128,384]{1,2,0:T(8,128)(2,1)}), bf16[8,128,384]{1,2,0:T(8,128)(2,1)}, u32[]{:S(2)}, u32[]{:S(2)}) async-start(bf16[8,128,384]{1,2,0:T(8,128)(2,1)} %fusion.47), calls=%async_computation.3 | async-start | bytes 1572864 | tf_op jit(solution)/shard_map/all_to_all | solution.py:110
  296.2 2.0 copy-start.8
  318.2 25.2 %all-to-all-start.4 = ((bf16[8,128,384]{2,1,0:T(8,128)(2,1)}), bf16[8,128,384]{2,1,0:T(8,128)(2,1)S(1)}, u32[]{:S(2)}, u32[]{:S(2)}) async-start(bf16[8,128,384]{2,1,0:T(8,128)(2,1)} %copy.163), calls=%async_computation.4 | async-start | bytes 1572864 | tf_op jit(solution)/shard_map/all_to_all | solution.py:113
  323.4 25.6 %copy-start.5 = (f32[8,128,384]{1,0,2:T(8,128)S(1)}, f32[8,128,384]{1,0,2:T(8,128)}, u32[]{:S(2)}) copy-start(f32[8,128,384]{1,0,2:T(8,128)} %copy-done.4) | copy-start | bytes 4718596
  343.4 5.5 %copy-start.9 = (bf16[8,128,384]{2,1,0:T(8,128)(2,1)}, bf16[8,128,384]{2,1,0:T(8,128)(2,1)S(1)}, u32[]{:S(2)}) copy-start(bf16[8,128,384]{2,1,0:T(8,128)(2,1)S(1)} %all-to-all-done.4) | copy-start | bytes 2359300
  343.4 25.9 %all-to-all-start.5 = ((bf16[8,128,384]{2,1,0:T(8,128)(2,1)}), bf16[8,128,384]{2,1,0:T(8,128)(2,1)}, u32[]{:S(2)}, u32[]{:S(2)}) async-start(bf16[8,128,384]{2,1,0:T(8,128)(2,1)} %copy.165), calls=%async_computation.5 | async-start | bytes 1572864 | tf_op jit(solution)/shard_map/all_to_all | solution.py:116
  349.0 1.9 copy-start.6
  353.6 2.4 copy-start.10
Sparse Core Ops, SparseCore 0:
  9.8 179.0 all-gather.2
  200.5 91.9 reduce-scatter.1
where the time goes:
time: 432 us; the launch traced here: 430 us
  waiting for transfers between devices  156 us (36%)
  matrix products  86.1 us (20%)
  local copies, waits for them, and re-layouts  60.2 us (14%)
  blocking collectives  43.5 us (10%)
  starting transfers between devices  36.9 us (9%)
  other arithmetic  26.9 us (6%)
  between operations  17.5 us (4%)
    psum x4, blocking collectives, one_axis_at_a_time(): array = lax.psum(array, axis)  43.5 us
    all_gather x1, waiting for transfers between devices, local(): out_full = lax.all_gather(out_grad[0], 'seq', axis=0, tiled=True)  32.1 us
    all_to_all x1, waiting for transfers between devices, local(): lax.all_to_all(key_rows[0], 'seq', split_axis=1, concat_axis=0, tiled=True)  30 us
    all_to_all x1, waiting for transfers between devices, local(): lax.all_to_all(query_rows[0], 'seq', split_axis=1, concat_axis=0, tiled=T...  26.2 us
    dot_general x2, matrix products, backward_block(): jnp.einsum('hqk,qhd->khd', d_scores, query_block, preferred_element_type=...  20.3 us
    all_to_all x1, waiting for transfers between devices, local(): lax.all_to_all(value_rows[0], 'seq', split_axis=1, concat_axis=0, tiled=T...  19.1 us
    dot_general x2, matrix products, backward_block(): jnp.einsum('hqk,khd->qhd', d_scores, k_norm, preferred_element_type=jnp.f...  19 us
    all_to_all x1, waiting for transfers between devices, local(): lax.all_to_all(key_grad.reshape(total, width), 'seq', split_axis=0, conca...  18.6 us
  transfers between devices with their start and end apart: 8, of which 7 were waited for; matrix products, arithmetic and copies ran while one was open for 35% of the time, Pallas kernels for 0%

commit v1 on v0

--- a/solution.py
+++ b/solution.py
@@ -9,6 +9,12 @@
 DP = ("dp_0", "dp_1", "dp_2")
 DP_SEQ = ("dp_0", "dp_1", "dp_2", "seq")
 EPS = 1e-06
+
+
+def gather_from_all(x, axis, dim):
+    size = lax.axis_size(axis)
+    repeats = [size if d == dim else 1 for d in range(x.ndim)]
+    return lax.all_to_all(jnp.tile(x, repeats), axis, split_axis=dim, concat_axis=dim, tiled=True)
 
 
 def one_axis_at_a_time(array, axes):
@@ -72,7 +78,7 @@
 
     probs_all, attn_blocks = lax.map(forward_block, jnp.arange(blocks, dtype=jnp.int32))
     attn_flat = attn_blocks.reshape(total, width)
-    out_full = lax.all_gather(out_grad[0], "seq", axis=0, tiled=True)
+    out_full = gather_from_all(out_grad[0], "seq", 0)
     weight_part = jnp.dot(attn_flat.T, out_full, preferred_element_type=jnp.float32)
     d_attn = jnp.dot(out_full, out_weight.T, preferred_element_type=jnp.float32).astype(
         jnp.bfloat16

time: 432 us -> 627 us (1.45)
  waiting for transfers between devices: 156 us -> 319 us
  blocking collectives: 43.5 us -> 68.4 us
  local copies, waits for them, and re-layouts: 60.2 us -> 67.7 us
    all_to_all x1, waiting for transfers between devices: 19.1 us -> 225 us  [gather_from_all(): lax.all_to_all(jnp.tile(x, repeats), axis, split_axis=dim, concat_axis=di...]
    all_gather x1 -> x0, waiting for transfers between devices: 32.1 us -> none  [local(): out_full = lax.all_gather(out_grad[0], 'seq', axis=0, tiled=True)]
    all_to_all x0 -> x1, blocking collectives: none -> 26.7 us  [local(): lax.all_to_all(value_rows[0], 'seq', split_axis=1, concat_axis=0, tiled=T...]
    all_to_all x1, waiting for transfers between devices: 30 us -> 21.8 us  [local(): lax.all_to_all(key_rows[0], 'seq', split_axis=1, concat_axis=0, tiled=True)]
    another operation x0 -> x1, local copies, waits for them, and re-layouts: none -> 7.45 us  [gather_from_all(): jnp.tile(x, repeats)]
  transfers between devices with their start and end apart: 8 -> 7, of which waited for: 7 -> 6; matrix products, arithmetic and copies ran while one was open for 35% -> 22% of each run, Pallas kernels for 0% -> 0%
where the time goes in v1:
time: 627 us; the launch traced here: 626 us
  waiting for transfers between devices  319 us (51%)
  matrix products  85.7 us (14%)
  blocking collectives  68.4 us (11%)
  local copies, waits for them, and re-layouts  67.7 us (11%)
  starting transfers between devices  37.2 us (6%)
  other arithmetic  26.9 us (4%)
  between operations  17.5 us (3%)
    all_to_all x1, waiting for transfers between devices, gather_from_all(): lax.all_to_all(jnp.tile(x, repeats), axis, split_axis=dim, concat_axis=di...  225 us
    psum x4, blocking collectives, one_axis_at_a_time(): array = lax.psum(array, axis)  41.8 us
    all_to_all x1, blocking collectives, local(): lax.all_to_all(value_rows[0], 'seq', split_axis=1, concat_axis=0, tiled=T...  26.7 us
    all_to_all x1, waiting for transfers between devices, local(): lax.all_to_all(key_rows[0], 'seq', split_axis=1, concat_axis=0, tiled=True)  21.8 us
    all_to_all x1, waiting for transfers between devices, local(): lax.all_to_all(query_rows[0], 'seq', split_axis=1, concat_axis=0, tiled=T...  20.5 us
    all_to_all x1, waiting for transfers between devices, local(): lax.all_to_all(key_grad.reshape(total, width), 'seq', split_axis=0, conca...  20.5 us
    dot_general x2, matrix products, backward_block(): jnp.einsum('hqk,qhd->khd', d_scores, query_block, preferred_element_type=...  20.1 us
    dot_general x2, matrix products, backward_block(): jnp.einsum('hqk,khd->qhd', d_scores, k_norm, preferred_element_type=jnp.f...  19.2 us
  transfers between devices with their start and end apart: 7, of which 6 were waited for; matrix products, arithmetic and copies ran while one was open for 22% of the time, Pallas kernels for 0%

profile of v1, /device:TPU:32, one launch (start us, length us, event | category | flops | bytes accessed | tf_op | source)
XLA Modules:
  0.0 625.8 jit_solution(12253247911826746633)
XLA Ops:
  7.2 2.4 copy.144
  9.5 8.6 %all-to-all-start = ((bf16[128,8,384]{0,2,1:T(8,128)(2,1)}), bf16[128,8,384]{0,2,1:T(8,128)(2,1)S(1)}, u32[]{:S(2)}, u32[]{:S(2)}) async-start(bf16[128,8,384]{0,2,1:T(8,128)(2,1)} %bitcast.4), calls=%async_computation | async-start | bytes 1572864 | tf_op jit(solution)/shard_map/all_to_all | solution.py:50
  19.3 20.5 %all-to-all-done = bf16[128,8,384]{0,2,1:T(8,128)(2,1)S(1)} async-done(((bf16[128,8,384]{0,2,1:T(8,128)(2,1)}), bf16[128,8,384]{0,2,1:T(8,128)(2,1)S(1)}, u32[]{:S(2)}, u32[]{:S(2)}) %all-to-all-start) | async-done | bytes 786464 | tf_op jit(solution)/shard_map/all_to_all | solution.py:50
  39.8 4.9 all-to-all-start.1
  45.1 21.8 %all-to-all-done.1 = bf16[128,8,384]{0,2,1:T(8,128)(2,1)S(1)} async-done(((bf16[128,8,384]{0,2,1:T(8,128)(2,1)}), bf16[128,8,384]{0,2,1:T(8,128)(2,1)S(1)}, u32[]{:S(2)}, u32[]{:S(2)}) %all-to-all-start.1) | async-done | bytes 786464 | tf_op jit(solution)/shard_map/all_to_all | solution.py:51
  66.8 26.7 %all_to_all.96 = bf16[128,8,384]{0,2,1:T(8,128)(2,1)} all-to-all(bf16[128,8,384]{0,2,1:T(8,128)(2,1)S(1)} %bitcast.150), channel_id=1, replica_groups=mesh['dp_0'=4,'dp_1'=4,'dp_2'=2,'seq'=8] {'seq'}, dimensions={1} | all-to-all | bytes 1572864 | tf_op jit(solution)/shard_map/all_to_all | solution.py:52
  93.5 7.5 %tile.9 = bf16[8,128,6144]{2,1,0:T(8,128)(2,1)} broadcast(bf16[128,6144]{1,0:T(8,128)(2,1)} %bitcast.158), dimensions={1,2} | broadcast | bytes 14155776 | tf_op jit(solution)/shard_map/tile | solution.py:17
  100.9 6.8 %all-to-all-start.3 = ((bf16[8,128,6144]{2,1,0:T(8,128)(2,1)}), bf16[8,128,6144]{2,1,0:T(8,128)(2,1)}, u32[]{:S(2)}, u32[]{:S(2)}) async-start(bf16[8,128,6144]{2,1,0:T(8,128)(2,1)} %tile.9), calls=%async_computation.3 | async-start | bytes 25165824 | tf_op jit(solution)/shard_map/all_to_all | solution.py:17
  109.1 1.6 reshape.189
  111.9 2.1 copy.147
  114.0 1.5 reshape.190
  117.3 2.3 copy.151
  119.6 2.5 copy.149
  122.1 2.2 reshape.184
  124.3 2.3 copy.152
  126.6 1.7 multiply_reduce_fusion.5
  129.6 21.3 %while.27 = (s32[]{:T(128)}, bf16[2,3,512,1024]{3,2,1,0:T(8,128)(2,1)}, bf16[2,512,3,128]{3,1,2,0:T(8,128)(2,1)}, s32[2]{0:T(128)S(1)}, s32[1024]{0:T(1024)S(1)}...) while((s32[]{:T(128)}, ...), condition=%wide.region_6.7_spmd, body=%wide.region_4.6_spmd.sunk | while | flops 817035776 | bytes 85746000 | solution.py:79
  131.3 3.4 fusion.67
  134.8 1.9 bitcast_dynamic-update-slice_fusion.2
  137.8 1.6 copy-done.1
  142.0 3.4 fusion.67
  145.5 1.9 bitcast_dynamic-update-slice_fusion.2
  148.5 1.6 copy-done.1
  151.0 3.0 copy.167
  154.0 2.2 copy.180
  156.3 1.5 copy.176
  157.8 224.9 %all-to-all-done.3 = bf16[8,128,6144]{2,1,0:T(8,128)(2,1)} async-done(((bf16[8,128,6144]{2,1,0:T(8,128)(2,1)}), bf16[8,128,6144]{2,1,0:T(8,128)(2,1)}, u32[]{:S(2)}, u32[]{:S(2)}) %all-to-all-start.3) | async-done | bytes 12582944 | tf_op jit(solution)/shard_map/all_to_all | solution.py:17
  382.7 10.2 %convolution_convert_fusion.2 = bf16[1024,384]{0,1:T(8,128)(2,1)} fusion(bf16[1024,6144]{1,0:T(8,128)(2,1)} %bitcast.13, bf16[384,6144]{1,0:T(8,128)(2,1)} %param.17), kind=kOutput, calls=%fused_computation.58 | convolution fusion | flops 4832231424 | bytes 18087936 | tf_op jit(solution)/shard_map/dot_general | solution.py:83
  392.9 11.2 %convolution_convert_fusion.1 = bf16[384,6144]{0,1:T(8,128)(2,1)} fusion(bf16[1024,384]{0,1:T(8,128)(2,1)S(1)} %bitcast.159, bf16[1024,6144]{1,0:T(8,128)(2,1)} %bitcast.13), kind=kOutput, calls=%fused_computation.41 | convolution fusion | flops 4834197504 | bytes 18087936 | tf_op jit(solution)/shard_map/dot_general | solution.py:82
  404.1 57.8 %while.28 = (s32[]{:T(128)}, f32[1024,3,128]{0,2,1:T(8,128)}, f32[1024,3,128]{0,2,1:T(8,128)S(1)}, f32[2,512,3,128]{3,1,2,0:T(8,128)}, s32[2]{0:T(128)S(1)}, /*i...) while((s32[]{:T(128)}, f32[1024,3,128]{0,2,1:T(8,128)}, ...), condition=%wide.region_9.10_spmd.clone, body=%wide.region_7.9_spmd.clone.sunk | while | flops 1634210816 | bytes 57019604 | solution.py:108
  405.4 4.9 fusion.75
  410.3 10.0 %bitcast_add_fusion.4 = f32[1024,3,128]{0,2,1:T(8,128)} fusion(f32[1024,3,128]{0,2,1:T(8,128)} %get-tuple-element.528, f32[3,512,1024]{2,1,0:T(8,128)} %fusion.75, bf16[2,3,512,1024]{3,2,1,0:T(8,128)(2,1)} %get-tuple-element.547, s32[]{:T(128)} %get-tuple-element.527, pred[]{:T(512)S(6)} %compare.3, bf16[1024,3,128]{0,2,1:T(8,128)(2,1)} %get-tuple-element.546, ...), kind=kOutput, calls=%fused_computation.26.clone.1 | convolution fusion | flops 414452224 | bytes 22414340 | tf_op jit(solution)/shard_map/while/body/eval_jaxpr/hqk,qhd->khd/dot_general | solution.py:101
  420.3 9.7 %fusion.76 = f32[2,512,3,128]{3,1,2,0:T(8,128)} fusion(f32[2,512,3,128]{3,1,2,0:T(8,128)} %get-tuple-element.530, s32[]{:T(128)} %get-tuple-element.527, bf16[1024,3,128]{2,0,1:T(8,128)(2,1)} %get-tuple-element.550, f32[3,512,1024]{2,1,0:T(8,128)} %fusion.75, bf16[2,3,512,1024]{3,2,1,0:T(8,128)(2,1)} %get-tuple-element.547), kind=kOutput, calls=%fused_computation.28.clone.1 | convolution fusion | flops 413665792 | bytes 20448768 | tf_op jit(solution)/shard_map/while/body/eval_jaxpr/hqk,khd->qhd/dot_general | solution.py:104
  429.9 3.0 bitcast_add_fusion.5
  434.2 5.0 fusion.75
  439.2 10.2 %bitcast_add_fusion.4 = f32[1024,3,128]{0,2,1:T(8,128)} fusion(f32[1024,3,128]{0,2,1:T(8,128)} %get-tuple-element.528, f32[3,512,1024]{2,1,0:T(8,128)} %fusion.75, bf16[2,3,512,1024]{3,2,1,0:T(8,128)(2,1)} %get-tuple-element.547, s32[]{:T(128)} %get-tuple-element.527, pred[]{:T(512)S(6)} %compare.3, bf16[1024,3,128]{0,2,1:T(8,128)(2,1)} %get-tuple-element.546, ...), kind=kOutput, calls=%fused_computation.26.clone.1 | convolution fusion | flops 414452224 | bytes 22414340 | tf_op jit(solution)/shard_map/while/body/eval_jaxpr/hqk,qhd->khd/dot_general | solution.py:101
  449.4 9.5 %fusion.76 = f32[2,512,3,128]{3,1,2,0:T(8,128)} fusion(f32[2,512,3,128]{3,1,2,0:T(8,128)} %get-tuple-element.530, s32[]{:T(128)} %get-tuple-element.527, bf16[1024,3,128]{2,0,1:T(8,128)(2,1)} %get-tuple-element.550, f32[3,512,1024]{2,1,0:T(8,128)} %fusion.75, bf16[2,3,512,1024]{3,2,1,0:T(8,128)(2,1)} %get-tuple-element.547), kind=kOutput, calls=%fused_computation.28.clone.1 | convolution fusion | flops 413665792 | bytes 20448768 | tf_op jit(solution)/shard_map/while/body/eval_jaxpr/hqk,khd->qhd/dot_general | solution.py:104
  458.9 2.9 bitcast_add_fusion.5
  461.9 3.7 copy.156
  465.6 2.7 copy.159
  468.3 3.1 copy.160
  471.4 2.3 multiply_reduce_fusion.3
  473.8 1.5 copy.177
  475.3 3.3 reshape.186
  478.6 4.3 fusion.40
  482.9 6.5 %all-to-all-start.4 = ((bf16[8,128,384]{1,2,0:T(8,128)(2,1)}), bf16[8,128,384]{1,2,0:T(8,128)(2,1)}, u32[]{:S(2)}, u32[]{:S(2)}) async-start(bf16[8,128,384]{1,2,0:T(8,128)(2,1)} %fusion.40), calls=%async_computation.4 | async-start | bytes 1572864 | tf_op jit(solution)/shard_map/all_to_all | solution.py:116
  489.4 2.0 multiply_reduce_fusion
  492.1 1.4 copy.163
  493.4 18.1 %all-to-all-done.4 = bf16[8,128,384]{1,2,0:T(8,128)(2,1)} async-done(((bf16[8,128,384]{1,2,0:T(8,128)(2,1)}), bf16[8,128,384]{1,2,0:T(8,128)(2,1)}, u32[]{:S(2)}, u32[]{:S(2)}) %all-to-all-start.4) | async-done | bytes 786464 | tf_op jit(solution)/shard_map/all_to_all | solution.py:116
  511.6 4.9 all-to-all-start.5
  516.8 1.4 copy.165
  518.2 20.5 %all-to-all-done.5 = bf16[8,128,384]{2,1,0:T(8,128)(2,1)S(1)} async-done(((bf16[8,128,384]{2,1,0:T(8,128)(2,1)}), bf16[8,128,384]{2,1,0:T(8,128)(2,1)S(1)}, u32[]{:S(2)}, u32[]{:S(2)}) %all-to-all-start.5) | async-done | bytes 786464 | tf_op jit(solution)/shard_map/all_to_all | solution.py:119
  538.6 5.5 all-to-all-start.6
  544.2 1.9 reshape.191
  546.1 2.6 multiply_reduce_fusion.1
  548.8 2.4 copy.170
  552.7 13.7 %all-to-all-done.6 = bf16[8,128,384]{2,1,0:T(8,128)(2,1)} async-done(((bf16[8,128,384]{2,1,0:T(8,128)(2,1)}), bf16[8,128,384]{2,1,0:T(8,128)(2,1)}, u32[]{:S(2)}, u32[]{:S(2)}) %all-to-all-start.6) | async-done | bytes 786464 | tf_op jit(solution)/shard_map/all_to_all | solution.py:122
  566.4 1.5 copy.166
  569.1 1.6 fusion.41
  570.7 11.3 %all-reduce.2 = (f32[]{:T(128)}, f32[128]{0:T(128)S(1)}, f32[128]{0:T(128)S(1)}) all-reduce(f32[]{:T(128)} %fusion.41, f32[128]{0:T(128)S(1)} %multiply_reduce_fusion.1, f32[128]{0:T(128)S(1)} %get-tuple-element.303), channel_id=1, replica_groups=mesh['dp_0'=4,'dp_1'=4,'dp_2'=2,'seq'=8] {'dp_0'}, use_global_device_ids=true, to_apply=%region_14.15 | all-reduce | flops 257 | bytes 2056 | tf_op jit(solution)/shard_map/psum | solution.py:22
  582.0 11.2 %all-reduce.1 = (f32[]{:T(128)}, f32[128]{0:T(128)S(1)}, f32[128]{0:T(128)S(1)}) all-reduce(f32[]{:T(128)} %get-tuple-element.347, f32[128]{0:T(128)S(1)} %get-tuple-element.348, f32[128]{0:T(128)S(1)} %get-tuple-element.349), channel_id=1, replica_groups=mesh['dp_0'=4,'dp_1'=4,'dp_2'=2,'seq'=8] {'dp_1'}, use_global_device_ids=true, to_apply=%region_15.16 | all-reduce | flops 257 | bytes 2056 | tf_op jit(solution)/shard_map/psum | solution.py:22
  593.2 3.1 all-reduce.3
  596.3 16.2 %all-reduce = (f32[]{:T(128)}, f32[128]{0:T(128)S(1)}, f32[128]{0:T(128)S(1)}) all-reduce(f32[]{:T(128)} %get-tuple-element.350, f32[128]{0:T(128)S(1)} %get-tuple-element.351, f32[128]{0:T(128)S(1)} %get-tuple-element.352), channel_id=1, replica_groups=mesh['dp_0'=4,'dp_1'=4,'dp_2'=2,'seq'=8] {'seq'}, use_global_device_ids=true, to_apply=%region_17.18 | all-reduce | flops 257 | bytes 2056 | tf_op jit(solution)/shard_map/psum | solution.py:22
  616.1 1.6 convert_multiply_fusion.15
  (96 shorter events, 20.0 us)
Async XLA Ops:
  7.2 10.9 %copy-start.12 = (bf16[1,128,3072]{2,1,0:T(8,128)(2,1)S(1)}, bf16[1,128,3072]{2,1,0:T(8,128)(2,1)}, u32[]{:S(2)}) copy-start(bf16[1,128,3072]{2,1,0:T(8,128)(2,1)} %param.13) | copy-start | bytes 2359300
  9.5 30.2 %all-to-all-start = ((bf16[128,8,384]{0,2,1:T(8,128)(2,1)}), bf16[128,8,384]{0,2,1:T(8,128)(2,1)S(1)}, u32[]{:S(2)}, u32[]{:S(2)}) async-start(bf16[128,8,384]{0,2,1:T(8,128)(2,1)} %bitcast.4), calls=%async_computation | async-start | bytes 1572864 | tf_op jit(solution)/shard_map/all_to_all | solution.py:50
  18.1 26.6 %copy-start.13 = (bf16[1,128,3072]{2,1,0:T(8,128)(2,1)S(1)}, bf16[1,128,3072]{2,1,0:T(8,128)(2,1)}, u32[]{:S(2)}) copy-start(bf16[1,128,3072]{2,1,0:T(8,128)(2,1)} %param.14) | copy-start | bytes 2359300
  39.8 68.3 %copy-start.7 = (bf16[128,8,384]{0,2,1:T(8,128)(2,1)}, bf16[128,8,384]{0,2,1:T(8,128)(2,1)S(1)}, u32[]{:S(2)}) copy-start(bf16[128,8,384]{0,2,1:T(8,128)(2,1)S(1)} %all-to-all-done) | copy-start | bytes 2359300
  39.8 27.1 %all-to-all-start.1 = ((bf16[128,8,384]{0,2,1:T(8,128)(2,1)}), bf16[128,8,384]{0,2,1:T(8,128)(2,1)S(1)}, u32[]{:S(2)}, u32[]{:S(2)}) async-start(bf16[128,8,384]{0,2,1:T(8,128)(2,1)} %bitcast.8), calls=%async_computation.1 | async-start | bytes 1572864 | tf_op jit(solution)/shard_map/all_to_all | solution.py:51
  66.8 34.1 %copy-start.11 = (bf16[128,8,384]{0,2,1:T(8,128)(2,1)}, bf16[128,8,384]{0,2,1:T(8,128)(2,1)S(1)}, u32[]{:S(2)}) copy-start(bf16[128,8,384]{0,2,1:T(8,128)(2,1)S(1)} %all-to-all-done.1) | copy-start | bytes 2359300
  100.9 6.8 %copy-start.19 = (s32[1,4]{1,0:T(1,128)S(1)}, s32[1,4]{1,0:T(1,128)}, u32[]{:S(2)}) copy-start(s32[1,4]{1,0:T(1,128)} %param.16) | copy-start | bytes 52
  100.9 7.1 %copy-start.18 = (f32[128]{0:T(128)S(1)}, f32[128]{0:T(128)}, u32[]{:S(2)}) copy-start(f32[128]{0:T(128)} %param.18) | copy-start | bytes 1540
  100.9 281.7 %all-to-all-start.3 = ((bf16[8,128,6144]{2,1,0:T(8,128)(2,1)}), bf16[8,128,6144]{2,1,0:T(8,128)(2,1)}, u32[]{:S(2)}, u32[]{:S(2)}) async-start(bf16[8,128,6144]{2,1,0:T(8,128)(2,1)} %tile.9), calls=%async_computation.3 | async-start | bytes 25165824 | tf_op jit(solution)/shard_map/all_to_all | solution.py:17
  107.7 461.4 %reduce-scatter.2.cloned.1.call-start = ((), (), s32[]{:S(2)}) async-start(), calls=%async_computation.8 | async-start | bytes 4866048 | tf_op jit(solution)/shard_map/reduce_scatter | solution.py:126
  109.1 2.8 copy-start.4
  115.5 0.7 copy-start.17
  126.6 1.9 copy-start.3
  131.3 3.4 copy-start
  134.8 1.9 copy-start.2
  134.8 1.9 copy-start.14
  136.7 2.7 copy-start.1
  139.4 0.9 copy-start.15
  142.0 3.4 copy-start
  145.4 1.9 copy-start.2
  145.4 1.9 copy-start.14
  147.4 2.7 copy-start.1
  150.1 0.9 copy-start.15
  382.7 10.2 %copy-start.16 = (bf16[48,8,2,512]{3,1,2,0:T(8,128)(2,1)S(1)}, bf16[48,8,2,512]{3,1,2,0:T(8,128)(2,1)}, u32[]{:S(2)}) copy-start(bf16[48,8,2,512]{3,1,2,0:T(8,128)(2,1)} %copy.180) | copy-start | bytes 2359300
  482.9 28.7 %all-to-all-start.4 = ((bf16[8,128,384]{1,2,0:T(8,128)(2,1)}), bf16[8,128,384]{1,2,0:T(8,128)(2,1)}, u32[]{:S(2)}, u32[]{:S(2)}) async-start(bf16[8,128,384]{1,2,0:T(8,128)(2,1)} %fusion.40), calls=%async_computation.4 | async-start | bytes 1572864 | tf_op jit(solution)/shard_map/all_to_all | solution.py:116
  489.4 2.0 copy-start.8
  511.6 27.0 %all-to-all-start.5 = ((bf16[8,128,384]{2,1,0:T(8,128)(2,1)}), bf16[8,128,384]{2,1,0:T(8,128)(2,1)S(1)}, u32[]{:S(2)}, u32[]{:S(2)}) async-start(bf16[8,128,384]{2,1,0:T(8,128)(2,1)} %copy.163), calls=%async_computation.5 | async-start | bytes 1572864 | tf_op jit(solution)/shard_map/all_to_all | solution.py:119
  516.8 27.4 %copy-start.5 = (f32[8,128,384]{1,0,2:T(8,128)S(1)}, f32[8,128,384]{1,0,2:T(8,128)}, u32[]{:S(2)}) copy-start(f32[8,128,384]{1,0,2:T(8,128)} %copy-done.4) | copy-start | bytes 4718596
  538.6 5.5 copy-start.9
  538.6 27.8 %all-to-all-start.6 = ((bf16[8,128,384]{2,1,0:T(8,128)(2,1)}), bf16[8,128,384]{2,1,0:T(8,128)(2,1)}, u32[]{:S(2)}, u32[]{:S(2)}) async-start(bf16[8,128,384]{2,1,0:T(8,128)(2,1)} %copy.165), calls=%async_computation.6 | async-start | bytes 1572864 | tf_op jit(solution)/shard_map/all_to_all | solution.py:122
  544.2 1.9 copy-start.6
  548.8 2.4 copy-start.10
Sparse Core Ops, SparseCore 0:
  404.2 89.8 reduce-scatter.1
